TPU v7x, 256 devices: a whole 4x4x8 slice. The times are simulated.
256 devices in a mesh: node: 8 (over z_lo, core), local: 32 (over y, x, z_hi).
Axes of the slice: x: 4, y: 4, z: 8 (z_hi: 2, z_lo: 4; z = z_hi * 4 + z_lo), core: 2. Of those that a mesh axis runs over, the one named last changes fastest.
Arguments:
- partials: bfloat16 [8, 32, 1048576], P('node', 'local'), may hold values from -8 to 8
- signs: int32 [1048576], replicated, may hold values 0 or 1
Outputs:
- reduced: float32 [1048576], P(('node', 'local'))
- rotated_max: float32 [8192], P(('node', 'local'))
Inputs may be any that keep to these rules, and one draw needn't show every extreme that they name: `signs`: 0 selects the sign +1 and 1 the sign -1 of a position.
All inputs are finite; a program needn't handle non-finite values.
Results may differ from a plain program's by a relative error of at most 0.0003.
Values may be sent and summed in bfloat16 or wider, within the bound.
A program may use at most 64 MiB of HBM per device.

v0:
```python
import jax
import jax.numpy as jnp
from jax import lax
from jax.sharding import PartitionSpec as P

ROT = 256
QGROUP = 128


def side_by_side(arrays, axis, split_dim, concat_dim, along):
    both = jnp.concatenate(arrays, axis=along)
    whole, at, done = (
        lax.all_to_all(both, axis, split_axis=split_dim, concat_axis=concat_dim, tiled=True),
        0,
        [],
    )
    for a in arrays:
        done.append(lax.slice_in_dim(whole, at, at + a.shape[along], axis=along))
        at += a.shape[along]
    return tuple(done)


def sylvester():
    positions = jnp.arange(ROT, dtype=jnp.int32)
    parity = jnp.zeros((ROT, ROT), dtype=jnp.int32)
    for level in range(ROT.bit_length() - 1):
        column = positions >> level & 1
        parity = parity + column[:, None] * column[None, :]
    return (1 - 2 * (parity % 2)).astype(jnp.float32)


def power_scale(largest):
    scaling = jnp.full(largest.shape, 2.0 ** (-37), dtype=jnp.float32)
    for power in range(-30, 31):
        scaling = jnp.where(largest >= 2.0**power, jnp.float32(2.0 ** (power - 7)), scaling)
    return scaling


def quantize(scaled):
    magnitude = jnp.abs(scaled)
    spacing = jnp.full(scaled.shape, 2.0 ** (-9), dtype=jnp.float32)
    for power in range(-5, 8):
        spacing = jnp.where(magnitude >= 2.0**power, jnp.float32(2.0 ** (power - 3)), spacing)
    return jnp.sign(scaled) * jnp.floor(magnitude / spacing + 0.5) * spacing


def encode(values):
    grouped = values.reshape(values.shape[:-1] + (values.shape[-1] // QGROUP, QGROUP))
    largest = jnp.max(jnp.abs(grouped), axis=-1)
    scaling = power_scale(largest)
    coded = quantize(grouped / scaling[..., None]).astype(jnp.bfloat16)
    return (coded.reshape(values.shape), scaling.astype(jnp.bfloat16))


def decode(coded, scales):
    grouped = coded.reshape(coded.shape[:-1] + (coded.shape[-1] // QGROUP, QGROUP))
    values = grouped.astype(jnp.float32) * scales.astype(jnp.float32)[..., None]
    return values.reshape(coded.shape)


def local_section(coded, scales):
    got_coded, got_scales = side_by_side((coded, scales), "local", 1, 1, 2)
    return encode(jnp.sum(decode(got_coded, got_scales), axis=1))


def shards(partials, signs):
    values = partials.reshape(-1)
    length = values.shape[0]
    members = lax.axis_size("local")
    groups = lax.axis_size("node")
    portion = length // (members * groups)
    matrix = sylvester()
    signed = values * (1 - 2 * signs).astype(jnp.bfloat16)
    rotated = jnp.dot(
        signed.reshape(-1, ROT), matrix.astype(jnp.bfloat16), preferred_element_type=jnp.float32
    ).reshape(-1)
    coded, scales = encode(rotated)
    coded = coded.reshape(groups, members, portion)
    scales = scales.reshape(groups, members, portion // QGROUP)
    first_coded, first_scales = local_section(coded, scales)
    far_coded, far_scales = side_by_side((first_coded, first_scales), "node", 0, 0, 1)
    second = jnp.sum(decode(far_coded, far_scales), axis=0)
    rotated_max = jnp.max(jnp.abs(second.reshape(-1, QGROUP)), axis=-1) / jnp.sqrt(jnp.float32(ROT))
    node_index = lax.axis_index("node")
    local_index = lax.axis_index("local")
    offset = node_index * (length // groups) + local_index * portion
    own_flips = (1 - 2 * lax.dynamic_slice_in_dim(signs, offset, portion)).astype(jnp.float32)
    turned_back = jnp.dot(
        second.reshape(-1, ROT),
        matrix,
        precision=lax.Precision.HIGHEST,
        preferred_element_type=jnp.float32,
    ).reshape(-1)
    reduced = turned_back / ROT * own_flips
    return (reduced, rotated_max)


def solution(mesh):
    in_specs = (P("node", "local", None), P())
    out_specs = (P(("node", "local")), P(("node", "local")))
    return jax.shard_map(shards, mesh=mesh, in_specs=in_specs, out_specs=out_specs, check_vma=False)
```

profile of v0, /device:TPU:1, one launch (start us, length us, event | category | flops | bytes accessed | tf_op | source)
XLA Modules:
  0.0 171.1 jit_solution(5664750579910854538)
XLA Ops:
  0.7 44.5 %reduce = bf16[1048576]{0:T(1024)(128)(2,1)S(1)} reduce(bf16[1,1,1048576]{2,1,0:T(2,128)(2,1)} %param.2, bf16[]{:T(256)} %constant.14), dimensions={0,1}, to_apply=%param.2.reduce_sub_computation | reduce | bytes 4194306 | tf_op args[0]
  45.2 4.3 %fusion.1 = bf16[1048576]{0:T(1024)(128)(2,1)} fusion(bf16[1048576]{0:T(1024)(128)(2,1)S(1)} %reduce, s32[1048576]{0:T(1024)} %param.3), kind=kLoop, calls=%fused_computation.14 | loop fusion | flops 4194304 | bytes 8388608 | tf_op jit(solution)/shard_map/mul | solution.py:73
  49.5 2.7 %reshape.492 = bf16[4096,256]{1,0:T(8,128)(2,1)S(1)} reshape(bf16[1048576]{0:T(1024)(128)(2,1)} %fusion.1) | data formatting | bytes 4194304 | tf_op jit(solution)/shard_map/reshape | solution.py:75
  52.2 4.2 %fusion.20 = (f32[4096,256]{1,0:T(8,128)}, f32[4096,256]{1,0:T(8,128)}) fusion(bf16[4096,256]{1,0:T(8,128)(2,1)S(1)} %reshape.492, s32[256]{0:T(256)S(1)} %get-tuple-element.53, s32[256]{0:T(256)S(1)} %get-tuple-element.54, s32[256]{0:T(256)S(1)} %get-tuple-element.55, s32[256]{0:T(256)S(1)} %get-tuple-element.56, s32[256]{0:T(256)S(1)} %get-tuple-element.57, ...), kind=kOutput, calls=%fused_computation.110 | convolution fusion | flops 539885568 | bytes 10493952 | tf_op jit(solution)/shard_map/dot_general | solution.py:74
  56.4 4.7 %abs.27 = f32[8192,128]{1,0:T(8,128)} reshape(f32[4096,256]{1,0:T(8,128)} %get-tuple-element.51) | data formatting | bytes 8388608 | tf_op jit(solution)/shard_map/abs | solution.py:49
  61.1 3.3 %reduce_max.27 = f32[8192]{0:T(1024)S(1)} reduce(f32[8192,128]{1,0:T(8,128)} %abs.27, f32[]{:T(128)} %constant.92.clone.1), dimensions={1}, to_apply=%region_0.1 | reduce | flops 1040384 | bytes 4227076 | tf_op jit(solution)/shard_map/reduce_max | solution.py:49
  64.5 0.2 broadcast_compare_fusion
  69.8 0.7 fusion.19
  70.5 0.2 copy.32
  70.7 5.0 %reshape_reshape.4 = f32[8,32,4096]{2,1,0:T(8,128)} reshape(f32[4096,256]{1,0:T(8,128)} %get-tuple-element.52) | data formatting | bytes 8388608 | tf_op jit(solution)/shard_map/reshape;reshape | solution.py:48
  75.7 8.4 %multiply_convert_fusion = bf16[8,32,4096]{2,0,1:T(8,128)(2,1)S(1)} fusion(f32[8,32,4096]{2,1,0:T(8,128)} %reshape_reshape.4, f32[8,32,32]{0,2,1:T(8,128)S(1)} %copy.32), kind=kLoop, calls=%fused_computation.3 | loop fusion | flops 36700160 | bytes 6324224 | tf_op jit(solution)/shard_map/convert_element_type | solution.py:51
  84.1 0.2 pad_maximum_fusion
  84.3 53.0 %all_to_all.17 = bf16[8,32,4128]{2,0,1:T(8,128)(2,1)S(1)} all-to-all(bf16[8,32,4128]{2,0,1:T(8,128)(2,1)S(1)} %pad_maximum_fusion), channel_id=1, replica_groups=mesh['node'=8,'local'=32] {'local'}, dimensions={1} | all-to-all | bytes 4227072 | tf_op jit(solution)/shard_map/all_to_all | solution.py:13
  137.4 0.2 copy.35
  137.6 1.3 fusion
  139.1 0.3 multiply_convert_fusion.1
  139.4 0.5 broadcast.1476
  139.9 0.7 reduce.1
  140.6 0.7 reshape.519
  141.3 21.8 %all-to-all-start.1 = ((bf16[8,2,2064]{2,1,0:T(2,128)(2,1)}), bf16[8,2,2064]{2,1,0:T(2,128)(2,1)S(1)}, u32[]{:S(2)}, u32[]{:S(2)}) async-start(bf16[8,2,2064]{2,1,0:T(2,128)(2,1)} %reshape.519), calls=%async_computation.1 | async-start | bytes 139264 | tf_op jit(solution)/shard_map/all_to_all | solution.py:13
  163.2 5.1 %all-to-all-done.1 = bf16[8,2,2064]{2,1,0:T(2,128)(2,1)S(1)} async-done(((bf16[8,2,2064]{2,1,0:T(2,128)(2,1)}), bf16[8,2,2064]{2,1,0:T(2,128)(2,1)S(1)}, u32[]{:S(2)}, u32[]{:S(2)}) %all-to-all-start.1) | async-done | bytes 66080 | tf_op jit(solution)/shard_map/all_to_all | solution.py:13
  168.7 0.5 fusion.2
  169.3 0.5 broadcast_multiply_fusion
  169.8 1.3 convert_multiply_fusion
  (66 shorter events, 5.5 us)
Async XLA Ops:
  141.3 26.9 %all-to-all-start.1 = ((bf16[8,2,2064]{2,1,0:T(2,128)(2,1)}), bf16[8,2,2064]{2,1,0:T(2,128)(2,1)S(1)}, u32[]{:S(2)}, u32[]{:S(2)}) async-start(bf16[8,2,2064]{2,1,0:T(2,128)(2,1)} %reshape.519), calls=%async_computation.1 | async-start | bytes 139264 | tf_op jit(solution)/shard_map/all_to_all | solution.py:13
where the time goes:
time: 172 us; the launch traced here: 171 us
  other arithmetic  66.1 us (38%)
  blocking collectives  53 us (31%)
  starting transfers between devices  21.8 us (13%)
  local copies, waits for them, and re-layouts  19.1 us (11%)
  waiting for transfers between devices  5.07 us (3%)
  matrix products  4.78 us (3%)
    all_to_all x1, blocking collectives, side_by_side(): lax.all_to_all(both, axis, split_axis=split_dim, concat_axis=concat_dim,...  53 us
    unnamed x1, other arithmetic  44.5 us
    all_to_all x1, starting transfers between devices, side_by_side(): lax.all_to_all(both, axis, split_axis=split_dim, concat_axis=concat_dim,...  21.8 us
    convert_element_type x2, other arithmetic, encode(): coded = quantize(grouped / scaling[..., None]).astype(jnp.bfloat16)  8.68 us
    all_to_all x1, waiting for transfers between devices, side_by_side(): lax.all_to_all(both, axis, split_axis=split_dim, concat_axis=concat_dim,...  5.07 us
    another operation x1, local copies, waits for them, and re-layouts, encode(): values.reshape(values.shape[:-1] + (values.shape[-1] // QGROUP, QGROUP))  4.97 us
    abs x1, local copies, waits for them, and re-layouts, encode(): largest = jnp.max(jnp.abs(grouped), axis=-1)  4.7 us
    ge x45, local copies, waits for them, and re-layouts, power_scale(): largest >= 2.0 ** power  4.55 us
  transfers between devices with their start and end apart: 1, of which 1 were waited for; matrix products, arithmetic and copies ran while one was open for 0% of the time, Pallas kernels for 0%

commit v1 on v0

v1 whole, which is shorter than its diff:
```python
import functools

import jax
import jax.numpy as jnp
from jax import lax
from jax.experimental import pallas as pl
from jax.experimental.pallas import tpu as pltpu
from jax.sharding import PartitionSpec as P

ROT = 256
QGROUP = 128
MESH = pl.DeviceIdType.MESH
NEAR_LAST = (2, 1, 3, 0)


def power_below(values):
    lifted = values * 2.0**23
    nearest = (values + lifted) - lifted
    return jnp.where(nearest > values, 0.5 * nearest, nearest)


def encode(values):
    largest = jnp.max(jnp.abs(values), axis=0, keepdims=True)
    power = power_below(jnp.clip(largest, 2.0**-30, 1.5 * 2.0**30))
    inverse = 1.0 / power
    lifted = inverse * 2.0**23
    inverse = (inverse + lifted) - lifted
    units = jnp.trunc(values * (inverse * 2.0**17))
    anchor = jnp.maximum(jnp.abs(units) * 2.0**20, 1.5 * 2.0**24)
    code = (units * (1.0 + 2.0**-20) + anchor) - anchor
    return code * (power * 2.0**-17)


def kernel(
    x_hbm,
    signs_hbm,
    out_ref,
    max_ref,
    x_in,
    signs_in,
    own_signs,
    matrix,
    rows,
    coded,
    got_a,
    part,
    got_b,
    pair,
    got_c,
    recoded,
    got_n,
    in_sem,
    a_send,
    a_recv,
    b_send,
    b_recv,
    c_send,
    c_recv,
    n_send,
    n_recv,
):
    node, local = lax.axis_index("node"), lax.axis_index("local")
    me_y, me_x, me_z = local // 8, lax.rem(local // 2, 4), lax.rem(local, 2)

    def ahead(place, step):
        return lax.rem(place + step, 4)

    def device(y, x, z):
        return (node, y * 8 + x * 2 + z)

    def place_z(own):
        return me_z if own else 1 - me_z

    first_of = (me_x, me_y)
    second_of = (me_y, me_x)

    def along_first(h, step):
        if h == 0:
            return device(me_y, ahead(me_x, step), me_z)
        return device(ahead(me_y, step), me_x, me_z)

    def along_second(h, step):
        return along_first(1 - h, step)

    barrier = pltpu.get_barrier_semaphore()
    for h in range(2):
        for step in range(1, 4):
            pl.semaphore_signal(barrier, inc=1, device_id=along_first(h, step), device_id_type=MESH)
    pl.semaphore_signal(barrier, inc=1, device_id=device(me_y, me_x, 1 - me_z), device_id_type=MESH)
    for step in range(1, 8):
        pl.semaphore_signal(
            barrier, inc=1, device_id=(lax.rem(node + step, 8), local), device_id_type=MESH
        )

    def tile_of(own, dy, dx):
        return ahead(me_y, dy) * 8 + ahead(me_x, dx) * 2 + place_z(own)

    def load(own, dy, dx):
        t = tile_of(own, dy, dx)
        return (
            pltpu.make_async_copy(x_hbm.at[:, t], x_in.at[t], in_sem.at[0, t]),
            pltpu.make_async_copy(signs_hbm.at[:, t], signs_in.at[t], in_sem.at[1, t]),
        )

    for own in range(2):
        for dy in NEAR_LAST:
            for dx in NEAR_LAST:
                for copy in load(own, dy, dx):
                    copy.start()
    own_copy = pltpu.make_async_copy(signs_hbm.at[node, local], own_signs, in_sem.at[0, 32])
    own_copy.start()

    i = lax.broadcasted_iota(jnp.int32, (ROT, ROT), 0)
    j = lax.broadcasted_iota(jnp.int32, (ROT, ROT), 1)
    odd = lax.population_count(i & j) & 1
    matrix[...] = (1 - 2 * odd).astype(jnp.float32).astype(jnp.bfloat16)

    def send_a(own, h, c, step):
        return pltpu.make_async_remote_copy(
            src_ref=coded.at[h, own, c, ahead(first_of[h], step)],
            dst_ref=got_a.at[h, own, c, step - 1],
            send_sem=a_send.at[h, own, c, step - 1],
            recv_sem=a_recv.at[h, own, c, step - 1],
            device_id=along_first(h, step),
            device_id_type=MESH,
        )

    def send_b(own, h, step):
        return pltpu.make_async_remote_copy(
            src_ref=part.at[h, own, ahead(second_of[h], step)],
            dst_ref=got_b.at[h, own, step - 1],
            send_sem=b_send.at[h, own, step - 1],
            recv_sem=b_recv.at[h, own, step - 1],
            device_id=along_second(h, step),
            device_id_type=MESH,
        )

    def send_c(h):
        return pltpu.make_async_remote_copy(
            src_ref=pair.at[h],
            dst_ref=got_c.at[h],
            send_sem=c_send.at[h],
            recv_sem=c_recv.at[h],
            device_id=device(me_y, me_x, 1 - me_z),
            device_id_type=MESH,
        )

    def send_n(step):
        to = lax.rem(node + step, 8)
        return pltpu.make_async_remote_copy(
            src_ref=recoded.at[to],
            dst_ref=got_n.at[step - 1],
            send_sem=n_send.at[step - 1],
            recv_sem=n_recv.at[step - 1],
            device_id=(to, local),
            device_id_type=MESH,
        )

    def rotate_row(own, dy):
        for dx in NEAR_LAST:
            for copy in load(own, dy, dx):
                copy.wait()
        for k, dx in enumerate(NEAR_LAST):
            t = tile_of(own, dy, dx)
            for g in range(8):
                for q in range(4):
                    v = x_in[t, g, :, pl.ds(q * 1024, 1024)].astype(jnp.float32).reshape(8, 128)
                    s = signs_in[t, g, pl.ds(q * 8, 8), :]
                    rows[k, pl.ds(g * 32 + q * 8, 8), :] = jnp.where(s == 0, v, -v)
        for k, dx in enumerate(NEAR_LAST):
            blocks = jnp.concatenate(
                [
                    rows[k, pl.ds(0, 128, 2), :].astype(jnp.bfloat16),
                    rows[k, pl.ds(1, 128, 2), :].astype(jnp.bfloat16),
                ],
                axis=1,
            )
            rotated = lax.dot_general(
                matrix[...],
                blocks,
                (((1,), (1,)), ((), ())),
                preferred_element_type=jnp.float32,
            )
            y, x = ahead(me_y, dy), ahead(me_x, dx)
            coded[0, own, y, x] = encode(rotated[:QGROUP]).astype(jnp.bfloat16)
            coded[1, own, x, y] = encode(rotated[QGROUP:]).astype(jnp.bfloat16)

    def send_row(own, dy):
        y = ahead(me_y, dy)
        for dx in NEAR_LAST[:3]:
            send_a(own, 0, y, dx).start()
        if dy:
            for dx in NEAR_LAST:
                send_a(own, 1, ahead(me_x, dx), dy).start()

    def add_first(own, h, c):
        for step in range(1, 4):
            send_a(own, h, c, step).wait_recv()
        total = coded[h, own, c, first_of[h]].astype(jnp.float32)
        for step in range(1, 4):
            total += got_a[h, own, c, step - 1].astype(jnp.float32)
        return total

    def reduce_first(own, step):
        for h in range(2):
            c = ahead(second_of[h], step)
            part[h, own, c] = add_first(own, h, c)
            if step:
                send_b(own, h, step).start()

    def reduce_second(own, h):
        for step in range(1, 4):
            send_b(own, h, step).wait_recv()
        total = part[h, own, second_of[h]]
        for step in range(1, 4):
            total += got_b[h, own, step - 1]
        return total

    for n, dy in enumerate(NEAR_LAST):
        rotate_row(0, dy)
        if n == 0:
            pl.semaphore_wait(barrier, 14)
        send_row(0, dy)
    for dy in NEAR_LAST:
        rotate_row(1, dy)
    reduce_first(0, 2)
    reduce_first(0, 1)
    send_row(1, 2)
    reduce_first(0, 3)
    reduce_first(0, 0)
    for dy in NEAR_LAST[1:]:
        send_row(1, dy)
    for h in range(2):
        pair[h] = reduce_second(0, h)
        send_c(h).start()
    for step in NEAR_LAST:
        reduce_first(1, step)
    for h in range(2):
        first = reduce_second(1, h)
        send_c(h).wait_recv()
        decoded = encode(first + got_c[h])
        recoded[:, h] = decoded.T.astype(jnp.bfloat16).reshape(8, 16, QGROUP)
    for step in range(1, 8):
        send_n(step).start()
    own_copy.wait()
    second = [recoded[node, h].astype(jnp.float32) for h in range(2)]
    for step in range(1, 8):
        send_n(step).wait_recv()
        for h in range(2):
            second[h] += got_n[step - 1, h].astype(jnp.float32)

    lane = lax.broadcasted_iota(jnp.int32, (16, 32), 1)
    block = lax.broadcasted_iota(jnp.int32, (16, 32), 0)
    widest = jnp.zeros((1, 32), jnp.float32)
    for h in range(2):
        most = jnp.max(jnp.abs(second[h]), axis=1, keepdims=True) * (1.0 / 16.0)
        widest += jnp.sum(jnp.where(lane == 2 * block + h, most, 0.0), axis=0, keepdims=True)
    max_ref[...] = widest

    whole = jnp.concatenate(second, axis=1)
    high = whole.astype(jnp.bfloat16)
    rest = whole - high.astype(jnp.float32)
    middle = rest.astype(jnp.bfloat16)
    low = (rest - middle.astype(jnp.float32)).astype(jnp.bfloat16)
    pieces = jnp.concatenate([high, middle, low], axis=0)
    back = jnp.dot(pieces, matrix[...], preferred_element_type=jnp.float32)
    back = ((back[32:48] + back[16:32]) + back[0:16]) * (1.0 / ROT)
    for h in range(2):
        s = own_signs[pl.ds(h, 16, 2), :]
        half = back[:, h * QGROUP : (h + 1) * QGROUP]
        out_ref[pl.ds(h, 16, 2), :] = jnp.where(s == 0, half, -half)

    for own in range(2):
        for h in range(2):
            for step in range(1, 4):
                for c in range(4):
                    send_a(own, h, c, step).wait_send()
                send_b(own, h, step).wait_send()
    for h in range(2):
        send_c(h).wait_send()
    for step in range(1, 8):
        send_n(step).wait_send()


def shards(partials, signs):
    dma = pltpu.SemaphoreType.DMA
    out, widest = pl.pallas_call(
        kernel,
        out_shape=(
            jax.ShapeDtypeStruct((32, QGROUP), jnp.float32),
            jax.ShapeDtypeStruct((1, 32), jnp.float32),
        ),
        in_specs=[pl.BlockSpec(memory_space=pl.ANY)] * 2,
        out_specs=(
            pl.BlockSpec(memory_space=pltpu.VMEM),
            pl.BlockSpec(memory_space=pltpu.VMEM),
        ),
        scratch_shapes=[
            pltpu.VMEM((32, 8, 1, 4096), jnp.bfloat16),
            pltpu.VMEM((32, 8, 32, QGROUP), jnp.int32),
            pltpu.VMEM((32, QGROUP), jnp.int32),
            pltpu.VMEM((ROT, ROT), jnp.bfloat16),
            pltpu.VMEM((4, ROT, QGROUP), jnp.float32),
            pltpu.VMEM((2, 2, 4, 4, QGROUP, QGROUP), jnp.bfloat16),
            pltpu.VMEM((2, 2, 4, 3, QGROUP, QGROUP), jnp.bfloat16),
            pltpu.VMEM((2, 2, 4, QGROUP, QGROUP), jnp.float32),
            pltpu.VMEM((2, 2, 3, QGROUP, QGROUP), jnp.float32),
            pltpu.VMEM((2, QGROUP, QGROUP), jnp.float32),
            pltpu.VMEM((2, QGROUP, QGROUP), jnp.float32),
            pltpu.VMEM((8, 2, 16, QGROUP), jnp.bfloat16),
            pltpu.VMEM((7, 2, 16, QGROUP), jnp.bfloat16),
            dma((2, 33)),
            dma((2, 2, 4, 3)),
            dma((2, 2, 4, 3)),
            dma((2, 2, 3)),
            dma((2, 2, 3)),
            dma((2,)),
            dma((2,)),
            dma((7,)),
            dma((7,)),
        ],
        compiler_params=pltpu.CompilerParams(collective_id=0, has_side_effects=True),
    )(partials.reshape(8, 32, 1, 4096), signs.reshape(8, 32, 32, QGROUP))
    return out.reshape(-1), widest.reshape(-1)


def solution(mesh):
    in_specs = (P("node", "local", None), P())
    out_specs = (P(("node", "local")), P(("node", "local")))
    return jax.shard_map(shards, mesh=mesh, in_specs=in_specs, out_specs=out_specs, check_vma=False)
```

time: 172 us -> 40.4 us (0.23)
  other arithmetic: 66.1 us -> 0 us
  blocking collectives: 53 us -> 0 us
  Pallas kernels: 0 us -> 37.1 us
  starting transfers between devices: 21.8 us -> 0 us
  local copies, waits for them, and re-layouts: 19.1 us -> 2.46 us
  waiting for transfers between devices: 5.07 us -> 0 us
  matrix products: 4.78 us -> 0 us
    all_to_all x1 -> x0, blocking collectives: 53 us -> none  [side_by_side(): lax.all_to_all(both, axis, split_axis=split_dim, concat_axis=concat_dim,...]
    unnamed x1 -> x0, other arithmetic: 44.5 us -> none
    pallas_call x0 -> x1, Pallas kernels: none -> 37.1 us  [shards(): pl.pallas_call(kernel, out_shape=(jax.ShapeDtypeStruct((32, QGROUP), jnp....]
    all_to_all x1 -> x0, starting transfers between devices: 21.8 us -> none  [side_by_side(): lax.all_to_all(both, axis, split_axis=split_dim, concat_axis=concat_dim,...]
    convert_element_type x6 -> x0, other arithmetic: 9.45 us -> none  [the longest x2 8.68 us: encode(): coded = quantize(grouped / scaling[..., None]).astype(jnp.bfloat16)]
    mul x2 -> x0, other arithmetic: 5.61 us -> none  [the longest x1 4.29 us: shards(): signed = values * (1 - 2 * signs).astype(jnp.bfloat16)]
    all_to_all x1 -> x0, waiting for transfers between devices: 5.07 us -> none  [side_by_side(): lax.all_to_all(both, axis, split_axis=split_dim, concat_axis=concat_dim,...]
    another operation x1 -> x0, local copies, waits for them, and re-layouts: 4.97 us -> none  [encode(): values.reshape(values.shape[:-1] + (values.shape[-1] // QGROUP, QGROUP))]
  transfers between devices with their start and end apart: 1 -> 0, of which waited for: 1 -> 0; matrix products, arithmetic and copies ran while one was open for 0% -> 0% of each run, Pallas kernels for 0% -> 0%
where the time goes in v1:
time: 40.4 us; the launch traced here: 40.2 us
  Pallas kernels  37.1 us (92%)
  local copies, waits for them, and re-layouts  2.46 us (6%)
  between operations  0.64 us (2%)
    pallas_call x1, Pallas kernels, shards(): pl.pallas_call(kernel, out_shape=(jax.ShapeDtypeStruct((32, QGROUP), jnp....  37.1 us
    unnamed x2, local copies, waits for them, and re-layouts  2.46 us

profile of v1, /device:TPU:1, one launch (start us, length us, event | category | flops | bytes accessed | tf_op | source)
XLA Modules:
  0.0 40.2 jit_solution(7668372058884508110)
XLA Ops:
  0.6 37.1 %shard_map.41 = (f32[32,128]{1,0:T(8,128)}, f32[1,32]{1,0:T(1,128)}) custom-call(bf16[8,32,1,4096]{3,2,1,0:T(2,128)(2,1)} %bitcast.4, s32[8,32,32,128]{3,2,1,0:T(8,128)} %bitcast.5), custom_call_target="tpu_custom_call" | custom-call | tf_op jit(solution)/shard_map/pallas_call | solution.py:287
  37.7 1.3 %copy.6 = f32[4096]{0:T(1024)} copy(f32[4096]{0:T(1024)} %bitcast.6) | data formatting | bytes 32768
  39.1 1.1 %copy.7 = f32[32]{0:T(128)} copy(f32[32]{0:T(128)} %bitcast.7) | data formatting | bytes 256

commit v2 on v1

--- a/solution.py
+++ b/solution.py
@@ -11,6 +11,7 @@
 QGROUP = 128
 MESH = pl.DeviceIdType.MESH
 NEAR_LAST = (2, 1, 3, 0)
+FAR_FIRST = (6, 7, 4, 5, 2, 3, 1)
 
 
 def power_below(values):
@@ -102,11 +103,12 @@
             pltpu.make_async_copy(signs_hbm.at[:, t], signs_in.at[t], in_sem.at[1, t]),
         )
 
-    for own in range(2):
-        for dy in NEAR_LAST:
-            for dx in NEAR_LAST:
-                for copy in load(own, dy, dx):
-                    copy.start()
+    def start_loads(own, dy):
+        for dx in NEAR_LAST:
+            for copy in load(own, dy, dx):
+                copy.start()
+
+    start_loads(0, NEAR_LAST[0])
     own_copy = pltpu.make_async_copy(signs_hbm.at[node, local], own_signs, in_sem.at[0, 32])
     own_copy.start()
 
@@ -145,29 +147,36 @@
             device_id_type=MESH,
         )
 
-    def send_n(step):
-        to = lax.rem(node + step, 8)
+    def send_n(h, k):
+        z, core = node // 2, lax.rem(node, 2)
+        if k & 4:
+            z = lax.rem(z + 2, 4)
+        if k & 2:
+            z = z + 1 - 2 * lax.rem(z, 2)
+        if k & 1:
+            core = 1 - core
+        to = 2 * z + core
         return pltpu.make_async_remote_copy(
-            src_ref=recoded.at[to],
-            dst_ref=got_n.at[step - 1],
-            send_sem=n_send.at[step - 1],
-            recv_sem=n_recv.at[step - 1],
+            src_ref=recoded.at[to, h],
+            dst_ref=got_n.at[k - 1, h],
+            send_sem=n_send.at[h, k - 1],
+            recv_sem=n_recv.at[h, k - 1],
             device_id=(to, local),
             device_id_type=MESH,
         )
 
-    def rotate_row(own, dy):
-        for dx in NEAR_LAST:
+    def rotate(own, dy, steps):
+        for dx in steps:
             for copy in load(own, dy, dx):
                 copy.wait()
-        for k, dx in enumerate(NEAR_LAST):
+        for k, dx in enumerate(steps):
             t = tile_of(own, dy, dx)
             for g in range(8):
                 for q in range(4):
                     v = x_in[t, g, :, pl.ds(q * 1024, 1024)].astype(jnp.float32).reshape(8, 128)
                     s = signs_in[t, g, pl.ds(q * 8, 8), :]
                     rows[k, pl.ds(g * 32 + q * 8, 8), :] = jnp.where(s == 0, v, -v)
-        for k, dx in enumerate(NEAR_LAST):
+        for k, dx in enumerate(steps):
             blocks = jnp.concatenate(
                 [
                     rows[k, pl.ds(0, 128, 2), :].astype(jnp.bfloat16),
@@ -185,12 +194,11 @@
             coded[0, own, y, x] = encode(rotated[:QGROUP]).astype(jnp.bfloat16)
             coded[1, own, x, y] = encode(rotated[QGROUP:]).astype(jnp.bfloat16)
 
-    def send_row(own, dy):
-        y = ahead(me_y, dy)
-        for dx in NEAR_LAST[:3]:
-            send_a(own, 0, y, dx).start()
-        if dy:
-            for dx in NEAR_LAST:
+    def send_tiles(own, dy, steps=NEAR_LAST):
+        for dx in steps:
+            if dx:
+                send_a(own, 0, ahead(me_y, dy), dx).start()
+            if dy:
                 send_a(own, 1, ahead(me_x, dx), dy).start()
 
     def add_first(own, h, c):
@@ -216,20 +224,27 @@
             total += got_b[h, own, step - 1]
         return total
 
-    for n, dy in enumerate(NEAR_LAST):
-        rotate_row(0, dy)
-        if n == 0:
-            pl.semaphore_wait(barrier, 14)
-        send_row(0, dy)
+    first_row, *other_rows = NEAR_LAST
+    rotate(0, first_row, NEAR_LAST[:2])
+    for own in range(2):
+        for dy in other_rows if own == 0 else NEAR_LAST:
+            start_loads(own, dy)
+    pl.semaphore_wait(barrier, 14)
+    send_tiles(0, first_row, NEAR_LAST[:2])
+    rotate(0, first_row, NEAR_LAST[2:])
+    send_tiles(0, first_row, NEAR_LAST[2:])
+    for dy in other_rows:
+        rotate(0, dy, NEAR_LAST)
+        send_tiles(0, dy)
     for dy in NEAR_LAST:
-        rotate_row(1, dy)
+        rotate(1, dy, NEAR_LAST)
     reduce_first(0, 2)
     reduce_first(0, 1)
-    send_row(1, 2)
+    send_tiles(1, 2)
     reduce_first(0, 3)
     reduce_first(0, 0)
     for dy in NEAR_LAST[1:]:
-        send_row(1, dy)
+        send_tiles(1, dy)
     for h in range(2):
         pair[h] = reduce_second(0, h)
         send_c(h).start()
@@ -240,20 +255,28 @@
         send_c(h).wait_recv()
         decoded = encode(first + got_c[h])
         recoded[:, h] = decoded.T.astype(jnp.bfloat16).reshape(8, 16, QGROUP)
-    for step in range(1, 8):
-        send_n(step).start()
+        for k in FAR_FIRST:
+            send_n(h, k).start()
     own_copy.wait()
+    for own in range(2):
+        for h in range(2):
+            for step in range(1, 4):
+                for c in range(4):
+                    send_a(own, h, c, step).wait_send()
+                send_b(own, h, step).wait_send()
+    for h in range(2):
+        send_c(h).wait_send()
     second = [recoded[node, h].astype(jnp.float32) for h in range(2)]
-    for step in range(1, 8):
-        send_n(step).wait_recv()
-        for h in range(2):
-            second[h] += got_n[step - 1, h].astype(jnp.float32)
+    for h in range(2):
+        for k in reversed(FAR_FIRST):
+            send_n(h, k).wait_recv()
+            second[h] += got_n[k - 1, h].astype(jnp.float32)
 
     lane = lax.broadcasted_iota(jnp.int32, (16, 32), 1)
     block = lax.broadcasted_iota(jnp.int32, (16, 32), 0)
     widest = jnp.zeros((1, 32), jnp.float32)
     for h in range(2):
-        most = jnp.max(jnp.abs(second[h]), axis=1, keepdims=True) * (1.0 / 16.0)
+        most = jnp.max(jnp.abs(second[h]), axis=1, keepdims=True)
         widest += jnp.sum(jnp.where(lane == 2 * block + h, most, 0.0), axis=0, keepdims=True)
     max_ref[...] = widest
 
@@ -264,32 +287,31 @@
     low = (rest - middle.astype(jnp.float32)).astype(jnp.bfloat16)
     pieces = jnp.concatenate([high, middle, low], axis=0)
     back = jnp.dot(pieces, matrix[...], preferred_element_type=jnp.float32)
-    back = ((back[32:48] + back[16:32]) + back[0:16]) * (1.0 / ROT)
+    back = (back[32:48] + back[16:32]) + back[0:16]
     for h in range(2):
         s = own_signs[pl.ds(h, 16, 2), :]
         half = back[:, h * QGROUP : (h + 1) * QGROUP]
         out_ref[pl.ds(h, 16, 2), :] = jnp.where(s == 0, half, -half)
 
-    for own in range(2):
-        for h in range(2):
-            for step in range(1, 4):
-                for c in range(4):
-                    send_a(own, h, c, step).wait_send()
-                send_b(own, h, step).wait_send()
-    for h in range(2):
-        send_c(h).wait_send()
-    for step in range(1, 8):
-        send_n(step).wait_send()
+    for h in range(2):
+        for k in FAR_FIRST:
+            send_n(h, k).wait_send()
+
+
+def finish(turned_ref, most_ref, out_ref, max_ref):
+    out_ref[...] = turned_ref[...] * (1.0 / ROT)
+    max_ref[...] = most_ref[...] * (1.0 / 16.0)
 
 
 def shards(partials, signs):
     dma = pltpu.SemaphoreType.DMA
-    out, widest = pl.pallas_call(
+    shapes = (
+        jax.ShapeDtypeStruct((32, QGROUP), jnp.float32),
+        jax.ShapeDtypeStruct((1, 32), jnp.float32),
+    )
+    turned, most = pl.pallas_call(
         kernel,
-        out_shape=(
-            jax.ShapeDtypeStruct((32, QGROUP), jnp.float32),
-            jax.ShapeDtypeStruct((1, 32), jnp.float32),
-        ),
+        out_shape=shapes,
         in_specs=[pl.BlockSpec(memory_space=pl.ANY)] * 2,
         out_specs=(
             pl.BlockSpec(memory_space=pltpu.VMEM),
@@ -316,11 +338,12 @@
             dma((2, 2, 3)),
             dma((2,)),
             dma((2,)),
-            dma((7,)),
-            dma((7,)),
+            dma((2, 7)),
+            dma((2, 7)),
         ],
         compiler_params=pltpu.CompilerParams(collective_id=0, has_side_effects=True),
     )(partials.reshape(8, 32, 1, 4096), signs.reshape(8, 32, 32, QGROUP))
+    out, widest = pl.pallas_call(finish, out_shape=shapes)(turned, most)
     return out.reshape(-1), widest.reshape(-1)
 
 

time: 40.4 us -> 39.3 us (0.973)
  local copies, waits for them, and re-layouts: 2.46 us -> 0 us
  Pallas kernels: 37.1 us -> 38.4 us
    unnamed x2 -> x0, local copies, waits for them, and re-layouts: 2.46 us -> none
    pallas_call x1 -> x2, Pallas kernels: 37.1 us -> 38.4 us  [the longest x1 37 us: shards(): pl.pallas_call(kernel, out_shape=shapes, in_specs=[pl.BlockSpec(memory_sp...]
where the time goes in v2:
time: 39.3 us; the launch traced here: 39 us
  Pallas kernels  38.4 us (98%)
  between operations  0.64 us (2%)
    pallas_call x1, Pallas kernels, shards(): pl.pallas_call(kernel, out_shape=shapes, in_specs=[pl.BlockSpec(memory_sp...  37 us
    pallas_call x1, Pallas kernels, shards(): out, widest = pl.pallas_call(finish, out_shape=shapes)(turned, most)  1.33 us

profile of v2, /device:TPU:1, one launch (start us, length us, event | category | flops | bytes accessed | tf_op | source)
XLA Modules:
  0.0 39.0 jit_solution(16796855451267098393)
XLA Ops:
  0.6 37.0 %shard_map.41 = (f32[32,128]{1,0:T(8,128)}, f32[1,32]{1,0:T(1,128)}) custom-call(bf16[8,32,1,4096]{3,2,1,0:T(2,128)(2,1)} %bitcast.4, s32[8,32,32,128]{3,2,1,0:T(8,128)} %bitcast.5), custom_call_target="tpu_custom_call" | custom-call | tf_op jit(solution)/shard_map/pallas_call | solution.py:312
  37.7 1.3 %shard_map.42 = (f32[32,128]{1,0:T(8,128)}, f32[1,32]{1,0:T(1,128)}) custom-call(f32[32,128]{1,0:T(8,128)} %get-tuple-element.6.turned_ref, f32[1,32]{1,0:T(1,128)} %get-tuple-element.7.most_ref), custom_call_target="tpu_custom_call" | custom-call | tf_op jit(solution)/shard_map/pallas_call | solution.py:346

commit v3 on v2

--- a/solution.py
+++ b/solution.py
@@ -11,6 +11,7 @@
 QGROUP = 128
 MESH = pl.DeviceIdType.MESH
 NEAR_LAST = (2, 1, 3, 0)
+LOADS = ((0, 2), (2, 4), (4, 8), (8, 12), (12, 16), (16, 32))
 FAR_FIRST = (6, 7, 4, 5, 2, 3, 1)
 
 
@@ -96,20 +97,27 @@
     def tile_of(own, dy, dx):
         return ahead(me_y, dy) * 8 + ahead(me_x, dx) * 2 + place_z(own)
 
-    def load(own, dy, dx):
-        t = tile_of(own, dy, dx)
-        return (
-            pltpu.make_async_copy(x_hbm.at[:, t], x_in.at[t], in_sem.at[0, t]),
-            pltpu.make_async_copy(signs_hbm.at[:, t], signs_in.at[t], in_sem.at[1, t]),
-        )
-
-    def start_loads(own, dy):
-        for dx in NEAR_LAST:
-            for copy in load(own, dy, dx):
-                copy.start()
-
-    start_loads(0, NEAR_LAST[0])
-    own_copy = pltpu.make_async_copy(signs_hbm.at[node, local], own_signs, in_sem.at[0, 32])
+    def slot_of(own, dy, dx):
+        return 16 * own + 4 * NEAR_LAST.index(dy) + NEAR_LAST.index(dx)
+
+    def start_loads(group):
+        first, last = LOADS[group]
+        for slot in range(first, last):
+            own, dy, dx = slot // 16, NEAR_LAST[slot // 4 % 4], NEAR_LAST[slot % 4]
+            t = tile_of(own, dy, dx)
+            pltpu.make_async_copy(x_hbm.at[:, t], x_in.at[slot], in_sem.at[0, group]).start()
+            pltpu.make_async_copy(
+                signs_hbm.at[:, t], signs_in.at[slot], in_sem.at[1, group]
+            ).start()
+
+    def wait_loads(group):
+        first, last = LOADS[group]
+        for n, buffer in enumerate((x_in, signs_in)):
+            whole = buffer.at[pl.ds(first, last - first)]
+            pltpu.make_async_copy(whole, whole, in_sem.at[n, group]).wait()
+
+    start_loads(0)
+    own_copy = pltpu.make_async_copy(signs_hbm.at[node, local], own_signs, in_sem.at[0, len(LOADS)])
     own_copy.start()
 
     i = lax.broadcasted_iota(jnp.int32, (ROT, ROT), 0)
@@ -121,8 +129,8 @@
         return pltpu.make_async_remote_copy(
             src_ref=coded.at[h, own, c, ahead(first_of[h], step)],
             dst_ref=got_a.at[h, own, c, step - 1],
-            send_sem=a_send.at[h, own, c, step - 1],
-            recv_sem=a_recv.at[h, own, c, step - 1],
+            send_sem=a_send,
+            recv_sem=a_recv.at[h, own, c],
             device_id=along_first(h, step),
             device_id_type=MESH,
         )
@@ -131,8 +139,8 @@
         return pltpu.make_async_remote_copy(
             src_ref=part.at[h, own, ahead(second_of[h], step)],
             dst_ref=got_b.at[h, own, step - 1],
-            send_sem=b_send.at[h, own, step - 1],
-            recv_sem=b_recv.at[h, own, step - 1],
+            send_sem=b_send,
+            recv_sem=b_recv.at[h, own],
             device_id=along_second(h, step),
             device_id_type=MESH,
         )
@@ -141,7 +149,7 @@
         return pltpu.make_async_remote_copy(
             src_ref=pair.at[h],
             dst_ref=got_c.at[h],
-            send_sem=c_send.at[h],
+            send_sem=c_send,
             recv_sem=c_recv.at[h],
             device_id=device(me_y, me_x, 1 - me_z),
             device_id_type=MESH,
@@ -158,19 +166,16 @@
         to = 2 * z + core
         return pltpu.make_async_remote_copy(
             src_ref=recoded.at[to, h],
-            dst_ref=got_n.at[k - 1, h],
-            send_sem=n_send.at[h, k - 1],
-            recv_sem=n_recv.at[h, k - 1],
+            dst_ref=got_n.at[h, k - 1],
+            send_sem=n_send,
+            recv_sem=n_recv.at[h],
             device_id=(to, local),
             device_id_type=MESH,
         )
 
     def rotate(own, dy, steps):
-        for dx in steps:
-            for copy in load(own, dy, dx):
-                copy.wait()
         for k, dx in enumerate(steps):
-            t = tile_of(own, dy, dx)
+            t = slot_of(own, dy, dx)
             for g in range(8):
                 for q in range(4):
                     v = x_in[t, g, :, pl.ds(q * 1024, 1024)].astype(jnp.float32).reshape(8, 128)
@@ -201,9 +206,11 @@
             if dy:
                 send_a(own, 1, ahead(me_x, dx), dy).start()
 
+    def wait_for(buffer, sem):
+        pltpu.make_async_copy(buffer, buffer, sem).wait()
+
     def add_first(own, h, c):
-        for step in range(1, 4):
-            send_a(own, h, c, step).wait_recv()
+        wait_for(got_a.at[h, own, c], a_recv.at[h, own, c])
         total = coded[h, own, c, first_of[h]].astype(jnp.float32)
         for step in range(1, 4):
             total += got_a[h, own, c, step - 1].astype(jnp.float32)
@@ -217,25 +224,27 @@
                 send_b(own, h, step).start()
 
     def reduce_second(own, h):
-        for step in range(1, 4):
-            send_b(own, h, step).wait_recv()
+        wait_for(got_b.at[h, own], b_recv.at[h, own])
         total = part[h, own, second_of[h]]
         for step in range(1, 4):
             total += got_b[h, own, step - 1]
         return total
 
     first_row, *other_rows = NEAR_LAST
+    wait_loads(0)
     rotate(0, first_row, NEAR_LAST[:2])
-    for own in range(2):
-        for dy in other_rows if own == 0 else NEAR_LAST:
-            start_loads(own, dy)
+    for group in range(1, len(LOADS)):
+        start_loads(group)
     pl.semaphore_wait(barrier, 14)
     send_tiles(0, first_row, NEAR_LAST[:2])
+    wait_loads(1)
     rotate(0, first_row, NEAR_LAST[2:])
     send_tiles(0, first_row, NEAR_LAST[2:])
-    for dy in other_rows:
+    for n, dy in enumerate(other_rows):
+        wait_loads(2 + n)
         rotate(0, dy, NEAR_LAST)
         send_tiles(0, dy)
+    wait_loads(5)
     for dy in NEAR_LAST:
         rotate(1, dy, NEAR_LAST)
     reduce_first(0, 2)
@@ -252,31 +261,26 @@
         reduce_first(1, step)
     for h in range(2):
         first = reduce_second(1, h)
-        send_c(h).wait_recv()
+        wait_for(got_c.at[h], c_recv.at[h])
         decoded = encode(first + got_c[h])
         recoded[:, h] = decoded.T.astype(jnp.bfloat16).reshape(8, 16, QGROUP)
         for k in FAR_FIRST:
             send_n(h, k).start()
     own_copy.wait()
-    for own in range(2):
-        for h in range(2):
-            for step in range(1, 4):
-                for c in range(4):
-                    send_a(own, h, c, step).wait_send()
-                send_b(own, h, step).wait_send()
-    for h in range(2):
-        send_c(h).wait_send()
+    wait_for(got_a, a_send)
+    wait_for(got_b, b_send)
+    wait_for(got_c, c_send)
     second = [recoded[node, h].astype(jnp.float32) for h in range(2)]
     for h in range(2):
+        wait_for(got_n.at[h], n_recv.at[h])
         for k in reversed(FAR_FIRST):
-            send_n(h, k).wait_recv()
-            second[h] += got_n[k - 1, h].astype(jnp.float32)
+            second[h] += got_n[h, k - 1].astype(jnp.float32)
 
     lane = lax.broadcasted_iota(jnp.int32, (16, 32), 1)
     block = lax.broadcasted_iota(jnp.int32, (16, 32), 0)
     widest = jnp.zeros((1, 32), jnp.float32)
     for h in range(2):
-        most = jnp.max(jnp.abs(second[h]), axis=1, keepdims=True)
+        most = jnp.max(jnp.abs(second[h]), axis=1, keepdims=True) * (1.0 / 16.0)
         widest += jnp.sum(jnp.where(lane == 2 * block + h, most, 0.0), axis=0, keepdims=True)
     max_ref[...] = widest
 
@@ -287,31 +291,31 @@
     low = (rest - middle.astype(jnp.float32)).astype(jnp.bfloat16)
     pieces = jnp.concatenate([high, middle, low], axis=0)
     back = jnp.dot(pieces, matrix[...], preferred_element_type=jnp.float32)
-    back = (back[32:48] + back[16:32]) + back[0:16]
+    back = ((back[32:48] + back[16:32]) + back[0:16]) * (1.0 / ROT)
     for h in range(2):
         s = own_signs[pl.ds(h, 16, 2), :]
         half = back[:, h * QGROUP : (h + 1) * QGROUP]
         out_ref[pl.ds(h, 16, 2), :] = jnp.where(s == 0, half, -half)
 
-    for h in range(2):
-        for k in FAR_FIRST:
-            send_n(h, k).wait_send()
-
-
-def finish(turned_ref, most_ref, out_ref, max_ref):
-    out_ref[...] = turned_ref[...] * (1.0 / ROT)
-    max_ref[...] = most_ref[...] * (1.0 / 16.0)
+    wait_for(got_n, n_send)
+
+
+def finish(turned_ref, most_ref, out_ref, max_ref, sem):
+    copies = (
+        pltpu.make_async_copy(turned_ref, out_ref, sem.at[0]),
+        pltpu.make_async_copy(most_ref, max_ref, sem.at[1]),
+    )
+    for copy in copies:
+        copy.start()
+    for copy in copies:
+        copy.wait()
 
 
 def shards(partials, signs):
     dma = pltpu.SemaphoreType.DMA
-    shapes = (
-        jax.ShapeDtypeStruct((32, QGROUP), jnp.float32),
-        jax.ShapeDtypeStruct((1, 32), jnp.float32),
-    )
     turned, most = pl.pallas_call(
         kernel,
-        out_shape=shapes,
+        out_shape=(pltpu.VMEM((32, QGROUP), jnp.float32), pltpu.VMEM((1, 32), jnp.float32)),
         in_specs=[pl.BlockSpec(memory_space=pl.ANY)] * 2,
         out_specs=(
             pl.BlockSpec(memory_space=pltpu.VMEM),
@@ -330,20 +334,32 @@
             pltpu.VMEM((2, QGROUP, QGROUP), jnp.float32),
             pltpu.VMEM((2, QGROUP, QGROUP), jnp.float32),
             pltpu.VMEM((8, 2, 16, QGROUP), jnp.bfloat16),
-            pltpu.VMEM((7, 2, 16, QGROUP), jnp.bfloat16),
-            dma((2, 33)),
-            dma((2, 2, 4, 3)),
-            dma((2, 2, 4, 3)),
-            dma((2, 2, 3)),
-            dma((2, 2, 3)),
+            pltpu.VMEM((2, 7, 16, QGROUP), jnp.bfloat16),
+            dma((2, len(LOADS) + 1)),
+            dma,
+            dma((2, 2, 4)),
+            dma,
+            dma((2, 2)),
+            dma,
             dma((2,)),
+            dma,
             dma((2,)),
-            dma((2, 7)),
-            dma((2, 7)),
         ],
         compiler_params=pltpu.CompilerParams(collective_id=0, has_side_effects=True),
     )(partials.reshape(8, 32, 1, 4096), signs.reshape(8, 32, 32, QGROUP))
-    out, widest = pl.pallas_call(finish, out_shape=shapes)(turned, most)
+    out, widest = pl.pallas_call(
+        finish,
+        out_shape=(
+            jax.ShapeDtypeStruct((32, QGROUP), jnp.float32),
+            jax.ShapeDtypeStruct((1, 32), jnp.float32),
+        ),
+        in_specs=[pl.BlockSpec(memory_space=pltpu.VMEM)] * 2,
+        out_specs=[pl.BlockSpec(memory_space=pl.ANY)] * 2,
+        scratch_shapes=[dma((2,))],
+    )(
+        pltpu.with_memory_space_constraint(turned, pltpu.VMEM),
+        pltpu.with_memory_space_constraint(most, pltpu.VMEM),
+    )
     return out.reshape(-1), widest.reshape(-1)
 
 

time: 39.3 us -> 36.3 us (0.924)
  Pallas kernels: 38.4 us -> 35.4 us
    pallas_call x2, Pallas kernels: 38.4 us -> 35.4 us  [the longest x1 34.8 us: shards(): pl.pallas_call(kernel, out_shape=(pltpu.VMEM((32, QGROUP), jnp.float32),...]
where the time goes in v3:
time: 36.3 us; the launch traced here: 36.1 us
  Pallas kernels  35.4 us (98%)
  between operations  0.64 us (2%)
    pallas_call x1, Pallas kernels, shards(): pl.pallas_call(kernel, out_shape=(pltpu.VMEM((32, QGROUP), jnp.float32),...  34.8 us

profile of v3, /device:TPU:1, one launch (start us, length us, event | category | flops | bytes accessed | tf_op | source)
XLA Modules:
  0.0 36.1 jit_solution(10967934452998411685)
XLA Ops:
  0.6 34.8 %shard_map.41 = (f32[32,128]{1,0:T(8,128)S(1)}, f32[1,32]{1,0:T(1,128)S(1)}) custom-call(bf16[8,32,1,4096]{3,2,1,0:T(2,128)(2,1)} %bitcast.4, s32[8,32,32,128]{3,2,1,0:T(8,128)} %bitcast.5), custom_call_target="tpu_custom_call" | custom-call | tf_op jit(solution)/shard_map/pallas_call | solution.py:316
  35.5 0.6 %shard_map.42 = (f32[32,128]{1,0:T(8,128)}, f32[1,32]{1,0:T(1,128)}) custom-call(f32[32,128]{1,0:T(8,128)S(1)} %get-tuple-element.6.turned_ref, f32[1,32]{1,0:T(1,128)S(1)} %get-tuple-element.7.most_ref), custom_call_target="tpu_custom_call" | custom-call | tf_op jit(solution)/shard_map/pallas_call | solution.py:350

commit v4 on v3

--- a/solution.py
+++ b/solution.py
@@ -12,6 +12,7 @@
 MESH = pl.DeviceIdType.MESH
 NEAR_LAST = (2, 1, 3, 0)
 LOADS = ((0, 2), (2, 4), (4, 8), (8, 12), (12, 16), (16, 32))
+PARTS = ((0, 0, 64), (0, 64, 64), (1, 0, 128))
 FAR_FIRST = (6, 7, 4, 5, 2, 3, 1)
 
 
@@ -125,32 +126,37 @@
     odd = lax.population_count(i & j) & 1
     matrix[...] = (1 - 2 * odd).astype(jnp.float32).astype(jnp.bfloat16)
 
-    def send_a(own, h, c, step):
+    def rows_of(p):
+        return pl.ds(PARTS[p][1], PARTS[p][2])
+
+    def send_a(p, h, c, step):
+        own = PARTS[p][0]
         return pltpu.make_async_remote_copy(
-            src_ref=coded.at[h, own, c, ahead(first_of[h], step)],
-            dst_ref=got_a.at[h, own, c, step - 1],
+            src_ref=coded.at[h, own, c, ahead(first_of[h], step), rows_of(p)],
+            dst_ref=got_a.at[h, own, c, step - 1, rows_of(p)],
             send_sem=a_send,
-            recv_sem=a_recv.at[h, own, c],
+            recv_sem=a_recv.at[h, p, c],
             device_id=along_first(h, step),
             device_id_type=MESH,
         )
 
-    def send_b(own, h, step):
+    def send_b(p, h, step):
+        own = PARTS[p][0]
         return pltpu.make_async_remote_copy(
-            src_ref=part.at[h, own, ahead(second_of[h], step)],
-            dst_ref=got_b.at[h, own, step - 1],
+            src_ref=part.at[h, own, ahead(second_of[h], step), rows_of(p)],
+            dst_ref=got_b.at[h, own, step - 1, rows_of(p)],
             send_sem=b_send,
-            recv_sem=b_recv.at[h, own],
+            recv_sem=b_recv.at[h, p],
             device_id=along_second(h, step),
             device_id_type=MESH,
         )
 
-    def send_c(h):
+    def send_c(p, h):
         return pltpu.make_async_remote_copy(
-            src_ref=pair.at[h],
-            dst_ref=got_c.at[h],
+            src_ref=pair.at[h, rows_of(p)],
+            dst_ref=got_c.at[h, rows_of(p)],
             send_sem=c_send,
-            recv_sem=c_recv.at[h],
+            recv_sem=c_recv.at[h, p],
             device_id=device(me_y, me_x, 1 - me_z),
             device_id_type=MESH,
         )
@@ -199,36 +205,45 @@
             coded[0, own, y, x] = encode(rotated[:QGROUP]).astype(jnp.bfloat16)
             coded[1, own, x, y] = encode(rotated[QGROUP:]).astype(jnp.bfloat16)
 
-    def send_tiles(own, dy, steps=NEAR_LAST):
+    def send_tiles(dy, steps):
         for dx in steps:
             if dx:
-                send_a(own, 0, ahead(me_y, dy), dx).start()
+                send_a(0, 0, ahead(me_y, dy), dx).start()
             if dy:
-                send_a(own, 1, ahead(me_x, dx), dy).start()
+                send_a(0, 1, ahead(me_x, dx), dy).start()
+
+    def send_chunk(p, step):
+        for to in NEAR_LAST[:3]:
+            for h in range(2):
+                send_a(p, h, ahead(second_of[h], step), to).start()
 
     def wait_for(buffer, sem):
         pltpu.make_async_copy(buffer, buffer, sem).wait()
 
-    def add_first(own, h, c):
-        wait_for(got_a.at[h, own, c], a_recv.at[h, own, c])
-        total = coded[h, own, c, first_of[h]].astype(jnp.float32)
-        for step in range(1, 4):
-            total += got_a[h, own, c, step - 1].astype(jnp.float32)
-        return total
-
-    def reduce_first(own, step):
+    def reduce_first(p, step):
+        own, rows = PARTS[p][0], rows_of(p)
         for h in range(2):
             c = ahead(second_of[h], step)
-            part[h, own, c] = add_first(own, h, c)
+            wait_for(got_a.at[h, own, c, pl.ds(0, 3), rows], a_recv.at[h, p, c])
+            total = coded[h, own, c, first_of[h], rows].astype(jnp.float32)
+            for k in range(3):
+                total += got_a[h, own, c, k, rows].astype(jnp.float32)
+            part[h, own, c, rows] = total
             if step:
-                send_b(own, h, step).start()
-
-    def reduce_second(own, h):
-        wait_for(got_b.at[h, own], b_recv.at[h, own])
-        total = part[h, own, second_of[h]]
-        for step in range(1, 4):
-            total += got_b[h, own, step - 1]
+                send_b(p, h, step).start()
+
+    def reduce_second(p, h):
+        own, rows = PARTS[p][0], rows_of(p)
+        wait_for(got_b.at[h, own, pl.ds(0, 3), rows], b_recv.at[h, p])
+        total = part[h, own, second_of[h], rows]
+        for k in range(3):
+            total += got_b[h, own, k, rows]
         return total
+
+    def exchange_z(p):
+        for h in range(2):
+            pair[h, rows_of(p)] = reduce_second(p, h)
+            send_c(p, h).start()
 
     first_row, *other_rows = NEAR_LAST
     wait_loads(0)
@@ -236,32 +251,35 @@
     for group in range(1, len(LOADS)):
         start_loads(group)
     pl.semaphore_wait(barrier, 14)
-    send_tiles(0, first_row, NEAR_LAST[:2])
+    send_tiles(first_row, NEAR_LAST[:2])
     wait_loads(1)
     rotate(0, first_row, NEAR_LAST[2:])
-    send_tiles(0, first_row, NEAR_LAST[2:])
+    send_tiles(first_row, NEAR_LAST[2:])
     for n, dy in enumerate(other_rows):
         wait_loads(2 + n)
         rotate(0, dy, NEAR_LAST)
-        send_tiles(0, dy)
+        send_tiles(dy, NEAR_LAST)
+    for step in NEAR_LAST:
+        send_chunk(1, step)
     wait_loads(5)
     for dy in NEAR_LAST:
         rotate(1, dy, NEAR_LAST)
-    reduce_first(0, 2)
-    reduce_first(0, 1)
-    send_tiles(1, 2)
-    reduce_first(0, 3)
-    reduce_first(0, 0)
-    for dy in NEAR_LAST[1:]:
-        send_tiles(1, dy)
-    for h in range(2):
-        pair[h] = reduce_second(0, h)
-        send_c(h).start()
+    for step in NEAR_LAST:
+        reduce_first(0, step)
+    send_chunk(2, 2)
     for step in NEAR_LAST:
         reduce_first(1, step)
-    for h in range(2):
-        first = reduce_second(1, h)
-        wait_for(got_c.at[h], c_recv.at[h])
+    send_chunk(2, 1)
+    exchange_z(0)
+    send_chunk(2, 3)
+    send_chunk(2, 0)
+    exchange_z(1)
+    for step in NEAR_LAST:
+        reduce_first(2, step)
+    for h in range(2):
+        first = reduce_second(2, h)
+        wait_for(got_c.at[h, rows_of(0)], c_recv.at[h, 0])
+        wait_for(got_c.at[h, rows_of(1)], c_recv.at[h, 1])
         decoded = encode(first + got_c[h])
         recoded[:, h] = decoded.T.astype(jnp.bfloat16).reshape(8, 16, QGROUP)
         for k in FAR_FIRST:
@@ -337,11 +355,11 @@
             pltpu.VMEM((2, 7, 16, QGROUP), jnp.bfloat16),
             dma((2, len(LOADS) + 1)),
             dma,
-            dma((2, 2, 4)),
+            dma((2, 3, 4)),
+            dma,
+            dma((2, 3)),
             dma,
             dma((2, 2)),
-            dma,
-            dma((2,)),
             dma,
             dma((2,)),
         ],

time: 36.3 us -> 35.8 us (0.986)
  no operation moved by 1% of the time
where the time goes in v4:
time: 35.8 us; the launch traced here: 35.7 us
  Pallas kernels  35.1 us (98%)
  between operations  0.64 us (2%)
    pallas_call x1, Pallas kernels, shards(): pl.pallas_call(kernel, out_shape=(pltpu.VMEM((32, QGROUP), jnp.float32),...  34.5 us

profile of v4, /device:TPU:1, one launch (start us, length us, event | category | flops | bytes accessed | tf_op | source)
XLA Modules:
  0.0 35.7 jit_solution(643887105802923547)
XLA Ops:
  0.6 34.5 %shard_map.41 = (f32[32,128]{1,0:T(8,128)S(1)}, f32[1,32]{1,0:T(1,128)S(1)}) custom-call(bf16[8,32,1,4096]{3,2,1,0:T(2,128)(2,1)} %bitcast.4, s32[8,32,32,128]{3,2,1,0:T(8,128)} %bitcast.5), custom_call_target="tpu_custom_call" | custom-call | tf_op jit(solution)/shard_map/pallas_call | solution.py:334
  35.1 0.6 %shard_map.42 = (f32[32,128]{1,0:T(8,128)}, f32[1,32]{1,0:T(1,128)}) custom-call(f32[32,128]{1,0:T(8,128)S(1)} %get-tuple-element.6.turned_ref, f32[1,32]{1,0:T(1,128)S(1)} %get-tuple-element.7.most_ref), custom_call_target="tpu_custom_call" | custom-call | tf_op jit(solution)/shard_map/pallas_call | solution.py:368

commit v5 on v4

--- a/solution.py
+++ b/solution.py
@@ -52,6 +52,7 @@
     got_c,
     recoded,
     got_n,
+    told,
     in_sem,
     a_send,
     a_recv,
@@ -85,14 +86,28 @@
     def along_second(h, step):
         return along_first(1 - h, step)
 
+    z_low, core = node // 2, lax.rem(node, 2)
     barrier = pltpu.get_barrier_semaphore()
+
+    def here(zl, to_core, to_local):
+        pl.semaphore_signal(
+            barrier, inc=1, device_id=(2 * zl + to_core, to_local), device_id_type=MESH
+        )
+
     for h in range(2):
         for step in range(1, 4):
-            pl.semaphore_signal(barrier, inc=1, device_id=along_first(h, step), device_id_type=MESH)
-    pl.semaphore_signal(barrier, inc=1, device_id=device(me_y, me_x, 1 - me_z), device_id_type=MESH)
-    for step in range(1, 8):
+            here(z_low, 0, along_first(h, step)[1])
+    for step in range(1, 4):
+        here(ahead(z_low, step), 1, local)
+    here(z_low, 1, me_y * 8 + me_x * 2 + 1 - me_z)
+
+    @pl.when(core == 1)
+    def _():
+        here(z_low, 0, local)
+
+    def tell_other_core():
         pl.semaphore_signal(
-            barrier, inc=1, device_id=(lax.rem(node + step, 8), local), device_id_type=MESH
+            told, inc=1, device_id=(2 * z_low + 1 - core, local), device_id_type=MESH
         )
 
     def tile_of(own, dy, dx):
@@ -162,14 +177,12 @@
         )
 
     def send_n(h, k):
-        z, core = node // 2, lax.rem(node, 2)
+        z = z_low
         if k & 4:
             z = lax.rem(z + 2, 4)
         if k & 2:
             z = z + 1 - 2 * lax.rem(z, 2)
-        if k & 1:
-            core = 1 - core
-        to = 2 * z + core
+        to = 2 * z + (1 - core if k & 1 else core)
         return pltpu.make_async_remote_copy(
             src_ref=recoded.at[to, h],
             dst_ref=got_n.at[h, k - 1],
@@ -250,7 +263,16 @@
     rotate(0, first_row, NEAR_LAST[:2])
     for group in range(1, len(LOADS)):
         start_loads(group)
-    pl.semaphore_wait(barrier, 14)
+
+    @pl.when(core == 0)
+    def _():
+        pl.semaphore_wait(barrier, 13)
+        tell_other_core()
+
+    @pl.when(core == 1)
+    def _():
+        pl.semaphore_wait(told, 1)
+
     send_tiles(first_row, NEAR_LAST[:2])
     wait_loads(1)
     rotate(0, first_row, NEAR_LAST[2:])
@@ -270,6 +292,16 @@
     for step in NEAR_LAST:
         reduce_first(1, step)
     send_chunk(2, 1)
+
+    @pl.when(core == 1)
+    def _():
+        pl.semaphore_wait(barrier, 8)
+        tell_other_core()
+
+    @pl.when(core == 0)
+    def _():
+        pl.semaphore_wait(told, 1)
+
     exchange_z(0)
     send_chunk(2, 3)
     send_chunk(2, 0)
@@ -353,6 +385,7 @@
             pltpu.VMEM((2, QGROUP, QGROUP), jnp.float32),
             pltpu.VMEM((8, 2, 16, QGROUP), jnp.bfloat16),
             pltpu.VMEM((2, 7, 16, QGROUP), jnp.bfloat16),
+            pltpu.SemaphoreType.REGULAR,
             dma((2, len(LOADS) + 1)),
             dma,
             dma((2, 3, 4)),

time: 35.8 us -> 34.9 us (0.975)
  Pallas kernels: 35.1 us -> 34.2 us
    pallas_call x1, Pallas kernels: 34.5 us -> 33.6 us  [shards(): pl.pallas_call(kernel, out_shape=(pltpu.VMEM((32, QGROUP), jnp.float32),...]
where the time goes in v5:
time: 34.9 us; the launch traced here: 34.8 us
  Pallas kernels  34.2 us (98%)
  between operations  0.64 us (2%)
    pallas_call x1, Pallas kernels, shards(): pl.pallas_call(kernel, out_shape=(pltpu.VMEM((32, QGROUP), jnp.float32),...  33.6 us

profile of v5, /device:TPU:1, one launch (start us, length us, event | category | flops | bytes accessed | tf_op | source)
XLA Modules:
  0.0 34.8 jit_solution(10769991752366574621)
XLA Ops:
  0.6 33.6 %shard_map.41 = (f32[32,128]{1,0:T(8,128)S(1)}, f32[1,32]{1,0:T(1,128)S(1)}) custom-call(bf16[8,32,1,4096]{3,2,1,0:T(2,128)(2,1)} %bitcast.4, s32[8,32,32,128]{3,2,1,0:T(8,128)} %bitcast.5), custom_call_target="tpu_custom_call" | custom-call | tf_op jit(solution)/shard_map/pallas_call | solution.py:366
  34.2 0.6 %shard_map.42 = (f32[32,128]{1,0:T(8,128)}, f32[1,32]{1,0:T(1,128)}) custom-call(f32[32,128]{1,0:T(8,128)S(1)} %get-tuple-element.6.turned_ref, f32[1,32]{1,0:T(1,128)S(1)} %get-tuple-element.7.most_ref), custom_call_target="tpu_custom_call" | custom-call | tf_op jit(solution)/shard_map/pallas_call | solution.py:401

commit v6 on v5

--- a/solution.py
+++ b/solution.py
@@ -233,6 +233,12 @@
     def wait_for(buffer, sem):
         pltpu.make_async_copy(buffer, buffer, sem).wait()
 
+    def send_near(side, *steps):
+        @pl.when(me_z == side)
+        def _():
+            for step in steps:
+                send_chunk(2, step)
+
     def reduce_first(p, step):
         own, rows = PARTS[p][0], rows_of(p)
         for h in range(2):
@@ -288,10 +294,10 @@
         rotate(1, dy, NEAR_LAST)
     for step in NEAR_LAST:
         reduce_first(0, step)
-    send_chunk(2, 2)
+    send_near(0, 2)
     for step in NEAR_LAST:
         reduce_first(1, step)
-    send_chunk(2, 1)
+    send_near(0, 1)
 
     @pl.when(core == 1)
     def _():
@@ -303,9 +309,10 @@
         pl.semaphore_wait(told, 1)
 
     exchange_z(0)
-    send_chunk(2, 3)
-    send_chunk(2, 0)
+    send_near(0, 3, 0)
+    send_near(1, 2)
     exchange_z(1)
+    send_near(1, 1, 3, 0)
     for step in NEAR_LAST:
         reduce_first(2, step)
     for h in range(2):

time: 34.9 us -> 34.7 us (level)
  no operation moved by 1% of the time
where the time goes in v6:
time: 34.7 us; the launch traced here: 34.6 us
  Pallas kernels  33.9 us (98%)
  between operations  0.64 us (2%)
    pallas_call x1, Pallas kernels, shards(): pl.pallas_call(kernel, out_shape=(pltpu.VMEM((32, QGROUP), jnp.float32),...  33.3 us

profile of v6, /device:TPU:1, one launch (start us, length us, event | category | flops | bytes accessed | tf_op | source)
XLA Modules:
  0.0 34.6 jit_solution(3188071440001243918)
XLA Ops:
  0.6 33.3 %shard_map.41 = (f32[32,128]{1,0:T(8,128)S(1)}, f32[1,32]{1,0:T(1,128)S(1)}) custom-call(bf16[8,32,1,4096]{3,2,1,0:T(2,128)(2,1)} %bitcast.4, s32[8,32,32,128]{3,2,1,0:T(8,128)} %bitcast.5), custom_call_target="tpu_custom_call" | custom-call | tf_op jit(solution)/shard_map/pallas_call | solution.py:373
  33.9 0.6 %shard_map.42 = (f32[32,128]{1,0:T(8,128)}, f32[1,32]{1,0:T(1,128)}) custom-call(f32[32,128]{1,0:T(8,128)S(1)} %get-tuple-element.6.turned_ref, f32[1,32]{1,0:T(1,128)S(1)} %get-tuple-element.7.most_ref), custom_call_target="tpu_custom_call" | custom-call | tf_op jit(solution)/shard_map/pallas_call | solution.py:408

commit v7 on v6

--- a/solution.py
+++ b/solution.py
@@ -96,14 +96,14 @@
 
     for h in range(2):
         for step in range(1, 4):
-            here(z_low, 0, along_first(h, step)[1])
+            here(z_low, 1, along_first(h, step)[1])
     for step in range(1, 4):
-        here(ahead(z_low, step), 1, local)
-    here(z_low, 1, me_y * 8 + me_x * 2 + 1 - me_z)
-
-    @pl.when(core == 1)
+        here(ahead(z_low, step), 0, local)
+    here(z_low, 0, me_y * 8 + me_x * 2 + 1 - me_z)
+
+    @pl.when(core == 0)
     def _():
-        here(z_low, 0, local)
+        here(z_low, 1, local)
 
     def tell_other_core():
         pl.semaphore_signal(
@@ -270,12 +270,12 @@
     for group in range(1, len(LOADS)):
         start_loads(group)
 
-    @pl.when(core == 0)
+    @pl.when(core == 1)
     def _():
         pl.semaphore_wait(barrier, 13)
         tell_other_core()
 
-    @pl.when(core == 1)
+    @pl.when(core == 0)
     def _():
         pl.semaphore_wait(told, 1)
 
@@ -299,20 +299,19 @@
         reduce_first(1, step)
     send_near(0, 1)
 
-    @pl.when(core == 1)
+    @pl.when(core == 0)
     def _():
         pl.semaphore_wait(barrier, 8)
         tell_other_core()
 
-    @pl.when(core == 0)
+    @pl.when(core == 1)
     def _():
         pl.semaphore_wait(told, 1)
 
     exchange_z(0)
     send_near(0, 3, 0)
-    send_near(1, 2)
     exchange_z(1)
-    send_near(1, 1, 3, 0)
+    send_near(1, 2, 1, 3, 0)
     for step in NEAR_LAST:
         reduce_first(2, step)
     for h in range(2):

time: 34.7 us -> 34.2 us (0.986)
  Pallas kernels: 33.9 us -> 33.5 us
    pallas_call x1, Pallas kernels: 33.3 us -> 32.8 us  [shards(): pl.pallas_call(kernel, out_shape=(pltpu.VMEM((32, QGROUP), jnp.float32),...]
where the time goes in v7:
time: 34.2 us; the launch traced here: 34.1 us
  Pallas kernels  33.5 us (98%)
  between operations  0.64 us (2%)
    pallas_call x1, Pallas kernels, shards(): pl.pallas_call(kernel, out_shape=(pltpu.VMEM((32, QGROUP), jnp.float32),...  32.8 us

profile of v7, /device:TPU:1, one launch (start us, length us, event | category | flops | bytes accessed | tf_op | source)
XLA Modules:
  0.0 34.1 jit_solution(10050405824207168234)
XLA Ops:
  0.6 32.8 %shard_map.41 = (f32[32,128]{1,0:T(8,128)S(1)}, f32[1,32]{1,0:T(1,128)S(1)}) custom-call(bf16[8,32,1,4096]{3,2,1,0:T(2,128)(2,1)} %bitcast.4, s32[8,32,32,128]{3,2,1,0:T(8,128)} %bitcast.5), custom_call_target="tpu_custom_call" | custom-call | tf_op jit(solution)/shard_map/pallas_call | solution.py:372
  33.5 0.6 %shard_map.42 = (f32[32,128]{1,0:T(8,128)}, f32[1,32]{1,0:T(1,128)}) custom-call(f32[32,128]{1,0:T(8,128)S(1)} %get-tuple-element.6.turned_ref, f32[1,32]{1,0:T(1,128)S(1)} %get-tuple-element.7.most_ref), custom_call_target="tpu_custom_call" | custom-call | tf_op jit(solution)/shard_map/pallas_call | solution.py:407

commit v8 on v7

--- a/solution.py
+++ b/solution.py
@@ -308,8 +308,8 @@
     def _():
         pl.semaphore_wait(told, 1)
 
+    send_near(0, 3, 0)
     exchange_z(0)
-    send_near(0, 3, 0)
     exchange_z(1)
     send_near(1, 2, 1, 3, 0)
     for step in NEAR_LAST:

time: 34.2 us -> 34.2 us (level)
  no operation moved by 1% of the time
where the time goes in v8:
time: 34.2 us; the launch traced here: 34.1 us
  Pallas kernels  33.5 us (98%)
  between operations  0.64 us (2%)
    pallas_call x1, Pallas kernels, shards(): pl.pallas_call(kernel, out_shape=(pltpu.VMEM((32, QGROUP), jnp.float32),...  32.8 us

profile of v8, /device:TPU:1, one launch (start us, length us, event | category | flops | bytes accessed | tf_op | source)
XLA Modules:
  0.0 34.1 jit_solution(7408340345351501574)
XLA Ops:
  0.6 32.8 %shard_map.41 = (f32[32,128]{1,0:T(8,128)S(1)}, f32[1,32]{1,0:T(1,128)S(1)}) custom-call(bf16[8,32,1,4096]{3,2,1,0:T(2,128)(2,1)} %bitcast.4, s32[8,32,32,128]{3,2,1,0:T(8,128)} %bitcast.5), custom_call_target="tpu_custom_call" | custom-call | tf_op jit(solution)/shard_map/pallas_call | solution.py:372
  33.5 0.6 %shard_map.42 = (f32[32,128]{1,0:T(8,128)}, f32[1,32]{1,0:T(1,128)}) custom-call(f32[32,128]{1,0:T(8,128)S(1)} %get-tuple-element.6.turned_ref, f32[1,32]{1,0:T(1,128)S(1)} %get-tuple-element.7.most_ref), custom_call_target="tpu_custom_call" | custom-call | tf_op jit(solution)/shard_map/pallas_call | solution.py:407
